TPU v7x, 32 devices: a whole 2x2x4 slice. The times are simulated.
32 devices in a mesh: gx: 4 (over z), gy: 8 (over y, x, core).
Axes of the slice: x: 2, y: 2, z: 4, core: 2. Of those that a mesh axis runs over, the one named last changes fastest.
Arguments:
- stored_vectors: bfloat16 [2, 16, 32, 4096], P(None, None, 'gx', 'gy'), may hold values from -4 to 4
- disorder: float32 [2, 32, 4096], P(None, 'gx', 'gy'), may hold values from -1.5 to 1.5
- vacancy: int32 [2, 32, 4096], P(None, 'gx', 'gy'), may hold values 0 or 1
- plan: int32 [32], replicated, may hold values from 0 to 31, as said below
Outputs:
- local_moments: float32 [4, 2, 32, 4096], P(None, None, 'gx', 'gy')
- trace_moments: float32 [4, 16], replicated
Inputs may be any that keep to these rules, and one draw needn't show every extreme that they name: plan is a permutation of 0 to 31; stored block b is held by the device at gy index b // 4. The 4 lattice blocks of one device come from 4 different devices, and the 4 stored blocks of one device go to 4 different devices.
All inputs are finite; a program needn't handle non-finite values. No bound on the sum of `vacancy` on one device may be relied on, other than what follows from the above.
Results may differ from a plain program's by a relative error of at most 0.0003.
Values may be sent and summed in bfloat16 or wider, within the bound.
A program may use at most 64 MiB of HBM per device.

v0:
```python
import jax
import jax.numpy as jnp
from jax import lax
from jax.sharding import PartitionSpec as P

BLOCK = 128
R = 16
TERMS = 4
HOP_NEAR = 1.0
HOP_NEXT = 0.3
TWIST_COS = 0.4535961214255773
TWIST_SIN = 0.8912073600614354
SPREAD = 6.5
NEAR_A = ((0, 0), (-1, 0), (0, -1))
NEAR_B = ((0, 0), (1, 0), (0, 1))
SECOND = ((1, 0), (-1, 1), (0, -1))


def extended(block, sides, width):
    for axis, dim in sides:
        count = lax.axis_size(axis)
        forward = [(i, i + 1) for i in range(count - 1)]
        forward.append((count - 1, 0))
        backward = [(target, source) for source, target in forward]
        low = lax.ppermute(
            lax.slice_in_dim(block, block.shape[dim] - width, None, axis=dim), axis, forward
        )
        high = lax.ppermute(lax.slice_in_dim(block, 0, width, axis=dim), axis, backward)
        block = jnp.concatenate([low, block, high], axis=dim)
    return block


def collect_sum(fetch, field, shifts):
    total = fetch(field, shifts[0])
    for shift in shifts[1:]:
        total = total + fetch(field, shift)
    return total


def hamilton(fetch, real, imag, onsite, keep):
    backs = tuple(((-a, -b) for a, b in SECOND))
    out_real = []
    out_imag = []
    for sublat, chiral, bonds in ((0, 1.0, NEAR_A), (1, -1.0, NEAR_B)):
        other = 1 - sublat
        near_real = collect_sum(fetch, real[other], bonds)
        forward_real = collect_sum(fetch, real[sublat], SECOND)
        backward_real = collect_sum(fetch, real[sublat], backs)
        centre_real = fetch(real[sublat], (0, 0))
        mixed_real = TWIST_COS * (forward_real + backward_real)
        mixed_imag = chiral * TWIST_SIN * (forward_real - backward_real)
        level = onsite[sublat][None]
        if imag is None:
            result_imag = HOP_NEXT * mixed_imag
        else:
            near_imag = collect_sum(fetch, imag[other], bonds)
            forward_imag = collect_sum(fetch, imag[sublat], SECOND)
            backward_imag = collect_sum(fetch, imag[sublat], backs)
            centre_imag = fetch(imag[sublat], (0, 0))
            mixed_real = mixed_real - chiral * TWIST_SIN * (forward_imag - backward_imag)
            mixed_imag = mixed_imag + TWIST_COS * (forward_imag + backward_imag)
            result_imag = level * centre_imag - HOP_NEAR * near_imag + HOP_NEXT * mixed_imag
        result_real = level * centre_real - HOP_NEAR * near_real + HOP_NEXT * mixed_real
        factor = keep[sublat][None] / SPREAD
        out_real.append(result_real * factor)
        out_imag.append(result_imag * factor)
    return (jnp.stack(out_real), jnp.stack(out_imag))


def local(stored_vectors, disorder, vacancy, plan):
    column = lax.axis_index("gy")
    columns = lax.axis_size("gy")
    vectors = stored_vectors.shape[1]
    width_x = stored_vectors.shape[2]
    width_y = stored_vectors.shape[3]
    blocks_here = width_y // BLOCK
    total_blocks = plan.shape[0]
    wanted = lax.dynamic_slice_in_dim(plan, column * blocks_here, blocks_here)
    pieces = stored_vectors.reshape(2, vectors, width_x, blocks_here, BLOCK)
    held = column * blocks_here + jnp.arange(blocks_here, dtype=jnp.int32)
    matches = (plan[None, :] == held[:, None]).astype(jnp.int32)
    target = jnp.sum(jnp.arange(total_blocks, dtype=jnp.int32)[None, :] * matches, axis=1)
    target_device = target // blocks_here
    sender = (jnp.arange(columns, dtype=jnp.int32)[:, None] == target_device[None, :]).astype(
        jnp.bfloat16
    )
    outgoing = jnp.einsum(
        "pb,srxbc->psrxc", sender, pieces, preferred_element_type=jnp.float32
    ).astype(jnp.bfloat16)
    incoming = lax.all_to_all(outgoing, "gy", split_axis=0, concat_axis=0, tiled=True)
    source_device = wanted // blocks_here
    picker = (jnp.arange(columns, dtype=jnp.int32)[None, :] == source_device[:, None]).astype(
        jnp.bfloat16
    )
    arranged = jnp.einsum("kp,psrxc->srxkc", picker, incoming, preferred_element_type=jnp.float32)
    lattice = arranged.reshape(2, vectors, width_x, width_y)
    keep = vacancy.astype(jnp.float32)
    start = lattice * keep[:, None]
    sites_total = 2 * width_x * lax.axis_size("gx") * width_y * columns

    def operate(real, imag):
        if imag is None:
            joined = real[None]
        else:
            joined = jnp.stack([real, imag])
        padded = extended(joined, (("gx", 3), ("gy", 4)), 1)

        def fetch(field, shift):
            return field[
                :, 1 + shift[0] : 1 + shift[0] + width_x, 1 + shift[1] : 1 + shift[1] + width_y
            ]

        padded_imag = None if imag is None else padded[1]
        return hamilton(fetch, padded[0], padded_imag, disorder, keep)

    locals_list = []
    partials = []

    def record(field_real):
        product = start * field_real
        locals_list.append(jnp.sum(product, axis=1) / R)
        partial_value = jnp.sum(product, axis=(0, 2, 3))
        partials.append(partial_value)

    previous_real, previous_imag = (start, None)
    current_real, current_imag = operate(start, None)
    record(current_real)
    for term in range(1, TERMS):
        image_real, image_imag = operate(current_real, current_imag)
        next_real = 2.0 * image_real - previous_real
        if previous_imag is None:
            next_imag = 2.0 * image_imag
        else:
            next_imag = 2.0 * image_imag - previous_imag
        previous_real, previous_imag = (current_real, current_imag)
        current_real, current_imag = (next_real, next_imag)
        record(current_real)
    summed = lax.psum(jnp.stack(partials), ("gx", "gy"))
    return (jnp.stack(locals_list), summed / sites_total)


def solution(mesh):
    placed = (P(None, None, "gx", "gy"), P(None, "gx", "gy"), P(None, "gx", "gy"), P())
    return jax.shard_map(
        local,
        mesh=mesh,
        in_specs=placed,
        out_specs=(P(None, None, "gx", "gy"), P()),
        check_vma=False,
    )
```

profile of v0, /device:TPU:0, one launch (start us, length us, event | category | flops | bytes accessed | tf_op | source)
XLA Modules:
  0.0 175.9 jit_solution(6712092812964053303)
XLA Ops:
  2.9 5.2 %all-to-all-start = ((bf16[8,2,16,8,128]{4,3,2,1,0:T(8,128)(2,1)}), bf16[8,2,16,8,128]{4,3,2,1,0:T(8,128)(2,1)S(1)}, u32[]{:S(2)}, u32[]{:S(2)}) async-start(bf16[8,2,16,8,128]{4,3,2,1,0:T(8,128)(2,1)} %copy.10), calls=%async_computation | async-start | bytes 1048576 | tf_op jit(solution)/shard_map/all_to_all | solution.py:90
  8.8 9.0 %all-to-all-done = bf16[8,2,16,8,128]{4,3,2,1,0:T(8,128)(2,1)S(1)} async-done(((bf16[8,2,16,8,128]{4,3,2,1,0:T(8,128)(2,1)}), bf16[8,2,16,8,128]{4,3,2,1,0:T(8,128)(2,1)S(1)}, u32[]{:S(2)}, u32[]{:S(2)}) %all-to-all-start) | async-done | bytes 524320 | tf_op jit(solution)/shard_map/all_to_all | solution.py:90
  20.3 2.2 %collective-permute-start.1 = (f32[1,2,16,1,512]{4,3,2,1,0:T(1,128)S(1)}, f32[1,2,16,1,512]{4,3,2,1,0:T(1,128)S(1)}, u32[]{:S(2)}, u32[]{:S(2)}) collective-permute-start(f32[1,2,16,1,512]{4,3,2,1,0:T(1,128)S(1)} %get-tuple-element.54), channel_id=1, source_target_pairs={{8,0},{16,8},{24,16},{0,24},{9,1},{17,9},{25,17},{1,25},{10,2},{18... | collective-permute-start | bytes 196616 | tf_op jit(solution)/shard_map/ppermute | solution.py:28
  22.5 2.3 %collective-permute-done = f32[1,2,16,1,512]{4,3,2,1,0:T(1,128)S(1)} collective-permute-done((f32[1,2,16,1,512]{4,3,2,1,0:T(1,128)S(1)}, f32[1,2,16,1,512]{4,3,2,1,0:T(1,128)S(1)}, u32[]{:S(2)}, u32[]{:S(2)}) %collective-permute-start) | collective-permute-done | bytes 65568 | tf_op jit(solution)/shard_map/ppermute | solution.py:25
  25.5 2.6 %collective-permute-start.3 = (f32[1,2,16,10,1]{4,3,2,1,0:T(8,128)S(1)}, f32[1,2,16,10,1]{4,3,2,1,0:T(8,128)S(1)}, u32[]{:S(2)}, u32[]{:S(2)}) collective-permute-start(f32[1,2,16,10,1]{4,3,2,1,0:T(8,128)S(1)} %get-tuple-element.48), channel_id=1, source_target_pairs={{1,0},{2,1},{3,2},{4,3},{5,4},{6,5},{7,6},{0,7},{9,8},{10,9},{11,1... | collective-permute-start | bytes 3848 | tf_op jit(solution)/shard_map/ppermute | solution.py:28
  28.1 6.8 %collective-permute-done.2 = f32[1,2,16,10,1]{4,3,2,1,0:T(8,128)S(1)} collective-permute-done((f32[1,2,16,10,1]{4,3,2,1,0:T(8,128)S(1)}, f32[1,2,16,10,1]{4,3,2,1,0:T(8,128)S(1)}, u32[]{:S(2)}, u32[]{:S(2)}) %collective-permute-start.2) | collective-permute-done | bytes 1312 | tf_op jit(solution)/shard_map/ppermute | solution.py:25
  38.0 3.2 %collective-permute-start.5 = (f32[2,2,16,1,512]{4,3,2,1,0:T(1,128)S(1)}, f32[2,2,16,1,512]{4,3,2,1,0:T(1,128)S(1)}, u32[]{:S(2)}, u32[]{:S(2)}) collective-permute-start(f32[2,2,16,1,512]{4,3,2,1,0:T(1,128)S(1)} %get-tuple-element.46), channel_id=1, source_target_pairs={{8,0},{16,8},{24,16},{0,24},{9,1},{17,9},{25,17},{1,25},{10,2},{18... | collective-permute-start | bytes 393224 | tf_op jit(solution)/shard_map/ppermute | solution.py:28
  41.2 4.0 %collective-permute-done.4 = f32[2,2,16,1,512]{4,3,2,1,0:T(1,128)S(1)} collective-permute-done((f32[2,2,16,1,512]{4,3,2,1,0:T(1,128)S(1)}, f32[2,2,16,1,512]{4,3,2,1,0:T(1,128)S(1)}, u32[]{:S(2)}, u32[]{:S(2)}) %collective-permute-start.4) | collective-permute-done | bytes 131104 | tf_op jit(solution)/shard_map/ppermute | solution.py:25
  45.8 2.6 %collective-permute-start.7 = (f32[2,2,16,10,1]{4,3,2,1,0:T(8,128)S(1)}, f32[2,2,16,10,1]{4,3,2,1,0:T(8,128)S(1)}, u32[]{:S(2)}, u32[]{:S(2)}) collective-permute-start(f32[2,2,16,10,1]{4,3,2,1,0:T(8,128)S(1)} %get-tuple-element.33), channel_id=1, source_target_pairs={{1,0},{2,1},{3,2},{4,3},{5,4},{6,5},{7,6},{0,7},{9,8},{10,9},{11,1... | collective-permute-start | bytes 7688 | tf_op jit(solution)/shard_map/ppermute | solution.py:28
  48.5 11.6 %collective-permute-done.6 = f32[2,2,16,10,1]{4,3,2,1,0:T(8,128)S(1)} collective-permute-done((f32[2,2,16,10,1]{4,3,2,1,0:T(8,128)S(1)}, f32[2,2,16,10,1]{4,3,2,1,0:T(8,128)S(1)}, u32[]{:S(2)}, u32[]{:S(2)}) %collective-permute-start.6) | collective-permute-done | bytes 2592 | tf_op jit(solution)/shard_map/ppermute | solution.py:25
  60.0 1.9 %pad_maximum_fusion = f32[2,2,16,10,514]{4,3,2,1,0:T(8,128)S(1)} fusion(f32[2,2,16,10,1]{4,3,2,1,0:T(8,128)S(1)} %collective-permute-done.7, f32[2,2,16,1,512]{4,3,2,1,0:T(1,128)S(1)} %collective-permute-done.5, f32[1,2,16,8,512]{4,3,2,1,0:T(8,128)S(1)} %maximum_bitcast_fusion.1, f32[1,2,16,8,512]{4,3,2,1,0:T(8,128)S(1)} %maximum_bitcast_fusion, ...), kind=kLoop, calls=%fused_computation | loop fusion | flops 1644800 | bytes 2631680 | tf_op jit(solution)/shard_map/concatenate | solution.py:29
  65.9 2.1 %collective-permute-start.8 = (f32[2,2,16,1,512]{4,3,2,1,0:T(1,128)S(1)}, f32[2,2,16,1,512]{4,3,2,1,0:T(1,128)S(1)}, u32[]{:S(2)}, u32[]{:S(2)}) collective-permute-start(f32[2,2,16,1,512]{4,3,2,1,0:T(1,128)S(1)} %get-tuple-element.43), channel_id=1, source_target_pairs={{0,8},{8,16},{16,24},{24,0},{1,9},{9,17},{17,25},{25,1},{2,10},{10... | collective-permute-start | bytes 393224 | tf_op jit(solution)/shard_map/ppermute | solution.py:25
  69.8 4.4 %collective-permute-done.8 = f32[2,2,16,1,512]{4,3,2,1,0:T(1,128)S(1)} collective-permute-done((f32[2,2,16,1,512]{4,3,2,1,0:T(1,128)S(1)}, f32[2,2,16,1,512]{4,3,2,1,0:T(1,128)S(1)}, u32[]{:S(2)}, u32[]{:S(2)}) %collective-permute-start.8) | collective-permute-done | bytes 131104 | tf_op jit(solution)/shard_map/ppermute | solution.py:25
  74.2 1.9 %collective-permute-done.9 = f32[2,2,16,1,512]{4,3,2,1,0:T(1,128)S(1)} collective-permute-done((f32[2,2,16,1,512]{4,3,2,1,0:T(1,128)S(1)}, f32[2,2,16,1,512]{4,3,2,1,0:T(1,128)S(1)}, u32[]{:S(2)}, u32[]{:S(2)}) %collective-permute-start.9) | collective-permute-done | bytes 131104 | tf_op jit(solution)/shard_map/ppermute | solution.py:28
  76.5 2.6 %collective-permute-start.11 = (f32[2,2,16,10,1]{4,3,2,1,0:T(8,128)S(1)}, f32[2,2,16,10,1]{4,3,2,1,0:T(8,128)S(1)}, u32[]{:S(2)}, u32[]{:S(2)}) collective-permute-start(f32[2,2,16,10,1]{4,3,2,1,0:T(8,128)S(1)} %get-tuple-element.31), channel_id=1, source_target_pairs={{1,0},{2,1},{3,2},{4,3},{5,4},{6,5},{7,6},{0,7},{9,8},{10,9},{11,1... | collective-permute-start | bytes 7688 | tf_op jit(solution)/shard_map/ppermute | solution.py:28
  79.2 12.5 %collective-permute-done.10 = f32[2,2,16,10,1]{4,3,2,1,0:T(8,128)S(1)} collective-permute-done((f32[2,2,16,10,1]{4,3,2,1,0:T(8,128)S(1)}, f32[2,2,16,10,1]{4,3,2,1,0:T(8,128)S(1)}, u32[]{:S(2)}, u32[]{:S(2)}) %collective-permute-start.10) | collective-permute-done | bytes 2592 | tf_op jit(solution)/shard_map/ppermute | solution.py:25
  98.9 3.2 %collective-permute-start.13 = (f32[2,2,16,1,512]{4,3,2,1,0:T(1,128)}, f32[2,2,16,1,512]{4,3,2,1,0:T(1,128)}, u32[]{:S(2)}, u32[]{:S(2)}) collective-permute-start(f32[2,2,16,1,512]{4,3,2,1,0:T(1,128)} %get-tuple-element.42), channel_id=1, source_target_pairs={{8,0},{16,8},{24,16},{0,24},{9,1},{17,9},{25,17},{1,25},{10,2},{18... | collective-permute-start | bytes 393224 | tf_op jit(solution)/shard_map/ppermute | solution.py:28
  107.0 2.1 %pad_maximum_fusion.7 = (f32[2,2,16,10,1]{4,3,2,1,0:T(8,128)}, f32[2,2,16,10,1]{4,3,2,1,0:T(8,128)}) fusion(f32[2,2,16,1,512]{4,3,2,1,0:T(1,128)} %collective-permute-done.13, f32[2,2,16,1,512]{4,3,2,1,0:T(1,128)} %collective-permute-done.12, f32[1,2,16,8,512]{4,3,2,1,0:T(8,128)S(1)} %fusion.5, f32[1,2,16,8,512]{4,3,2,1,0:T(8,128)S(1)} %fusion.4), kind=kLoop, calls=%fused_computation.23 | loop fusion | flops 3840 | bytes 1315840 | tf_op jit(solution)/shard_map/slice | solution.py:26
  109.1 2.6 %collective-permute-start.15 = (f32[2,2,16,10,1]{4,3,2,1,0:T(8,128)}, f32[2,2,16,10,1]{4,3,2,1,0:T(8,128)}, u32[]{:S(2)}, u32[]{:S(2)}) collective-permute-start(f32[2,2,16,10,1]{4,3,2,1,0:T(8,128)} %get-tuple-element.29), channel_id=1, source_target_pairs={{1,0},{2,1},{3,2},{4,3},{5,4},{6,5},{7,6},{0,7},{9,8},{10,9},{11,1... | collective-permute-start | bytes 7688 | tf_op jit(solution)/shard_map/ppermute | solution.py:28
  115.1 9.4 %collective-permute-done.14 = f32[2,2,16,10,1]{4,3,2,1,0:T(8,128)} collective-permute-done((f32[2,2,16,10,1]{4,3,2,1,0:T(8,128)}, f32[2,2,16,10,1]{4,3,2,1,0:T(8,128)}, u32[]{:S(2)}, u32[]{:S(2)}) %collective-permute-start.14) | collective-permute-done | bytes 2592 | tf_op jit(solution)/shard_map/ppermute | solution.py:25
  124.5 3.1 %pad_maximum_fusion.2 = f32[2,2,16,10,514]{4,3,2,1,0:T(8,128)S(1)} fusion(f32[2,2,16,10,1]{4,3,2,1,0:T(8,128)} %collective-permute-done.15, f32[2,2,16,1,512]{4,3,2,1,0:T(1,128)} %collective-permute-done.13, f32[1,2,16,8,512]{4,3,2,1,0:T(8,128)S(1)} %fusion.5, f32[1,2,16,8,512]{4,3,2,1,0:T(8,128)S(1)} %fusion.4, ...), kind=kLoop, calls=%fused_computation.2 | loop fusion | flops 1644800 | bytes 2631680 | tf_op jit(solution)/shard_map/concatenate | solution.py:29
  129.5 2.4 %fusion.14 = f32[16,8,512]{2,1,0:T(8,128)} fusion(f32[16,10,514]{2,1,0:T(8,128)S(1)} %get-tuple-element.17, f32[16,10,514]{2,1,0:T(8,128)S(1)} %get-tuple-element.18, f32[16,10,514]{2,1,0:T(8,128)S(1)} %get-tuple-element.19, f32[8,512]{1,0:T(8,128)S(1)} %get-tuple-element.60, f32[8,512]{1,0:T(8,128)} %copy-done.5), kind=kLoop, calls=%fused_computation.58 | loop fusion | flops 1310720 | bytes 4489216 | tf_op jit(solution)/shard_map/mul | solution.py:65
  132.9 2.0 %fusion.38 = (f32[16]{0:T(128)S(1)}, f32[2,8,4,128]{3,2,1,0:T(4,128)S(1)}, f32[2,16,8,4,128]{4,3,2,1,0:T(4,128)S(1)}, f32[2,16,8,4,128]{4,3,2,1,0:T(4,128)S(1)}, f32[2,16,8,4,128]{4,3,2,1,0:T(4,128)S(1)}) fusion(f32[2,16,8,4,128]{4,3,2,1,0:T(4,128)S(1)} %copy-done.2, f32[2,16,8,4,128]{4,3,2,1,0:T(4,128)S(1)} %convolution_bitcast_fusion, ...), kind=kLoop, calls=%fused_computation.148 | loop fusion | flops 2088944 | bytes 4259904 | tf_op jit(solution)/shard_map/reduce_sum | solution.py:122
  135.7 38.9 %psum.7 = f32[4,16]{1,0:T(4,128)S(1)} all-reduce(f32[4,16]{1,0:T(4,128)S(1)} %pad_maximum_fusion.26), channel_id=1, replica_groups=mesh['gx'=4,'gy'=8] {'gx','gy'}, use_global_device_ids=true, to_apply=%region_9.10 | all-reduce | flops 64 | bytes 512 | tf_op jit(solution)/shard_map/psum | solution.py:138
  (103 shorter events, 36.0 us)
Async XLA Ops:
  0.6 7.5 %copy-start.9 = (s32[32]{0:T(128)S(1)}, s32[32]{0:T(128)}, u32[]{:S(2)}) copy-start(s32[32]{0:T(128)} %param.7) | copy-start | bytes 388
  0.7 7.6 %copy-start.7 = (s32[2,8,512]{2,1,0:T(8,128)S(1)}, s32[2,8,512]{2,1,0:T(8,128)}, u32[]{:S(2)}) copy-start(s32[2,8,512]{2,1,0:T(8,128)} %param.6) | copy-start | bytes 98308
  2.0 20.5 %copy-start.8 = (f32[2,8,512]{2,1,0:T(8,128)S(1)}, f32[2,8,512]{2,1,0:T(8,128)}, u32[]{:S(2)}) copy-start(f32[2,8,512]{2,1,0:T(8,128)} %param.5) | copy-start | bytes 98308
  2.9 14.9 %all-to-all-start = ((bf16[8,2,16,8,128]{4,3,2,1,0:T(8,128)(2,1)}), bf16[8,2,16,8,128]{4,3,2,1,0:T(8,128)(2,1)S(1)}, u32[]{:S(2)}, u32[]{:S(2)}) async-start(bf16[8,2,16,8,128]{4,3,2,1,0:T(8,128)(2,1)} %copy.10), calls=%async_computation | async-start | bytes 1048576 | tf_op jit(solution)/shard_map/all_to_all | solution.py:90
  18.6 6.2 %collective-permute-start = (f32[1,2,16,1,512]{4,3,2,1,0:T(1,128)S(1)}, f32[1,2,16,1,512]{4,3,2,1,0:T(1,128)S(1)}, u32[]{:S(2)}, u32[]{:S(2)}) collective-permute-start(f32[1,2,16,1,512]{4,3,2,1,0:T(1,128)S(1)} %get-tuple-element.53), channel_id=1, source_target_pairs={{0,8},{8,16},{16,24},{24,0},{1,9},{9,17},{17,25},{25,1},{2,10},{10... | collective-permute-start | bytes 196616 | tf_op jit(solution)/shard_map/ppermute | solution.py:25
  20.3 5.0 %collective-permute-start.1 = (f32[1,2,16,1,512]{4,3,2,1,0:T(1,128)S(1)}, f32[1,2,16,1,512]{4,3,2,1,0:T(1,128)S(1)}, u32[]{:S(2)}, u32[]{:S(2)}) collective-permute-start(f32[1,2,16,1,512]{4,3,2,1,0:T(1,128)S(1)} %get-tuple-element.54), channel_id=1, source_target_pairs={{8,0},{16,8},{24,16},{0,24},{9,1},{17,9},{25,17},{1,25},{10,2},{18... | collective-permute-start | bytes 196616 | tf_op jit(solution)/shard_map/ppermute | solution.py:28
  22.5 73.8 %copy-start.5 = (f32[8,512]{1,0:T(8,128)}, f32[8,512]{1,0:T(8,128)S(1)}, u32[]{:S(2)}) copy-start(f32[8,512]{1,0:T(8,128)S(1)} %get-tuple-element.66) | copy-start | bytes 49156
  25.4 9.6 %collective-permute-start.2 = (f32[1,2,16,10,1]{4,3,2,1,0:T(8,128)S(1)}, f32[1,2,16,10,1]{4,3,2,1,0:T(8,128)S(1)}, u32[]{:S(2)}, u32[]{:S(2)}) collective-permute-start(f32[1,2,16,10,1]{4,3,2,1,0:T(8,128)S(1)} %get-tuple-element.47), channel_id=1, source_target_pairs={{0,1},{1,2},{2,3},{3,4},{4,5},{5,6},{6,7},{7,0},{8,9},{9,10},{10,1... | collective-permute-start | bytes 3848 | tf_op jit(solution)/shard_map/ppermute | solution.py:25
  25.5 9.5 %collective-permute-start.3 = (f32[1,2,16,10,1]{4,3,2,1,0:T(8,128)S(1)}, f32[1,2,16,10,1]{4,3,2,1,0:T(8,128)S(1)}, u32[]{:S(2)}, u32[]{:S(2)}) collective-permute-start(f32[1,2,16,10,1]{4,3,2,1,0:T(8,128)S(1)} %get-tuple-element.48), channel_id=1, source_target_pairs={{1,0},{2,1},{3,2},{4,3},{5,4},{6,5},{7,6},{0,7},{9,8},{10,9},{11,1... | collective-permute-start | bytes 3848 | tf_op jit(solution)/shard_map/ppermute | solution.py:28
  37.3 7.9 %collective-permute-start.4 = (f32[2,2,16,1,512]{4,3,2,1,0:T(1,128)S(1)}, f32[2,2,16,1,512]{4,3,2,1,0:T(1,128)S(1)}, u32[]{:S(2)}, u32[]{:S(2)}) collective-permute-start(f32[2,2,16,1,512]{4,3,2,1,0:T(1,128)S(1)} %get-tuple-element.45), channel_id=1, source_target_pairs={{0,8},{8,16},{16,24},{24,0},{1,9},{9,17},{17,25},{25,1},{2,10},{10... | collective-permute-start | bytes 393224 | tf_op jit(solution)/shard_map/ppermute | solution.py:25
  38.0 7.4 %collective-permute-start.5 = (f32[2,2,16,1,512]{4,3,2,1,0:T(1,128)S(1)}, f32[2,2,16,1,512]{4,3,2,1,0:T(1,128)S(1)}, u32[]{:S(2)}, u32[]{:S(2)}) collective-permute-start(f32[2,2,16,1,512]{4,3,2,1,0:T(1,128)S(1)} %get-tuple-element.46), channel_id=1, source_target_pairs={{8,0},{16,8},{24,16},{0,24},{9,1},{17,9},{25,17},{1,25},{10,2},{18... | collective-permute-start | bytes 393224 | tf_op jit(solution)/shard_map/ppermute | solution.py:28
  45.8 14.2 %collective-permute-start.6 = (f32[2,2,16,10,1]{4,3,2,1,0:T(8,128)S(1)}, f32[2,2,16,10,1]{4,3,2,1,0:T(8,128)S(1)}, u32[]{:S(2)}, u32[]{:S(2)}) collective-permute-start(f32[2,2,16,10,1]{4,3,2,1,0:T(8,128)S(1)} %get-tuple-element.32), channel_id=1, source_target_pairs={{0,1},{1,2},{2,3},{3,4},{4,5},{5,6},{6,7},{7,0},{8,9},{9,10},{10,1... | collective-permute-start | bytes 7688 | tf_op jit(solution)/shard_map/ppermute | solution.py:25
  45.8 14.2 %collective-permute-start.7 = (f32[2,2,16,10,1]{4,3,2,1,0:T(8,128)S(1)}, f32[2,2,16,10,1]{4,3,2,1,0:T(8,128)S(1)}, u32[]{:S(2)}, u32[]{:S(2)}) collective-permute-start(f32[2,2,16,10,1]{4,3,2,1,0:T(8,128)S(1)} %get-tuple-element.33), channel_id=1, source_target_pairs={{1,0},{2,1},{3,2},{4,3},{5,4},{6,5},{7,6},{0,7},{9,8},{10,9},{11,1... | collective-permute-start | bytes 7688 | tf_op jit(solution)/shard_map/ppermute | solution.py:28
  65.9 8.3 %collective-permute-start.8 = (f32[2,2,16,1,512]{4,3,2,1,0:T(1,128)S(1)}, f32[2,2,16,1,512]{4,3,2,1,0:T(1,128)S(1)}, u32[]{:S(2)}, u32[]{:S(2)}) collective-permute-start(f32[2,2,16,1,512]{4,3,2,1,0:T(1,128)S(1)} %get-tuple-element.43), channel_id=1, source_target_pairs={{0,8},{8,16},{16,24},{24,0},{1,9},{9,17},{17,25},{25,1},{2,10},{10... | collective-permute-start | bytes 393224 | tf_op jit(solution)/shard_map/ppermute | solution.py:25
  68.0 8.1 %collective-permute-start.9 = (f32[2,2,16,1,512]{4,3,2,1,0:T(1,128)S(1)}, f32[2,2,16,1,512]{4,3,2,1,0:T(1,128)S(1)}, u32[]{:S(2)}, u32[]{:S(2)}) collective-permute-start(f32[2,2,16,1,512]{4,3,2,1,0:T(1,128)S(1)} %get-tuple-element.44), channel_id=1, source_target_pairs={{8,0},{16,8},{24,16},{0,24},{9,1},{17,9},{25,17},{1,25},{10,2},{18... | collective-permute-start | bytes 393224 | tf_op jit(solution)/shard_map/ppermute | solution.py:28
  76.5 15.2 %collective-permute-start.10 = (f32[2,2,16,10,1]{4,3,2,1,0:T(8,128)S(1)}, f32[2,2,16,10,1]{4,3,2,1,0:T(8,128)S(1)}, u32[]{:S(2)}, u32[]{:S(2)}) collective-permute-start(f32[2,2,16,10,1]{4,3,2,1,0:T(8,128)S(1)} %get-tuple-element.30), channel_id=1, source_target_pairs={{0,1},{1,2},{2,3},{3,4},{4,5},{5,6},{6,7},{7,0},{8,9},{9,10},{10,1... | collective-permute-start | bytes 7688 | tf_op jit(solution)/shard_map/ppermute | solution.py:25
  76.5 15.1 %collective-permute-start.11 = (f32[2,2,16,10,1]{4,3,2,1,0:T(8,128)S(1)}, f32[2,2,16,10,1]{4,3,2,1,0:T(8,128)S(1)}, u32[]{:S(2)}, u32[]{:S(2)}) collective-permute-start(f32[2,2,16,10,1]{4,3,2,1,0:T(8,128)S(1)} %get-tuple-element.31), channel_id=1, source_target_pairs={{1,0},{2,1},{3,2},{4,3},{5,4},{6,5},{7,6},{0,7},{9,8},{10,9},{11,1... | collective-permute-start | bytes 7688 | tf_op jit(solution)/shard_map/ppermute | solution.py:28
  97.2 4.9 %copy-start.6 = (f32[2,8,4,128]{3,1,2,0:T(8,128)S(1)}, f32[2,8,4,128]{3,1,2,0:T(8,128)}, u32[]{:S(2)}) copy-start(f32[2,8,4,128]{3,1,2,0:T(8,128)} %get-tuple-element.55) | copy-start | bytes 98308
  98.3 8.5 %collective-permute-start.12 = (f32[2,2,16,1,512]{4,3,2,1,0:T(1,128)}, f32[2,2,16,1,512]{4,3,2,1,0:T(1,128)}, u32[]{:S(2)}, u32[]{:S(2)}) collective-permute-start(f32[2,2,16,1,512]{4,3,2,1,0:T(1,128)} %get-tuple-element.41), channel_id=1, source_target_pairs={{0,8},{8,16},{16,24},{24,0},{1,9},{9,17},{17,25},{25,1},{2,10},{10... | collective-permute-start | bytes 393224 | tf_op jit(solution)/shard_map/ppermute | solution.py:25
  98.9 8.1 %collective-permute-start.13 = (f32[2,2,16,1,512]{4,3,2,1,0:T(1,128)}, f32[2,2,16,1,512]{4,3,2,1,0:T(1,128)}, u32[]{:S(2)}, u32[]{:S(2)}) collective-permute-start(f32[2,2,16,1,512]{4,3,2,1,0:T(1,128)} %get-tuple-element.42), channel_id=1, source_target_pairs={{8,0},{16,8},{24,16},{0,24},{9,1},{17,9},{25,17},{1,25},{10,2},{18... | collective-permute-start | bytes 393224 | tf_op jit(solution)/shard_map/ppermute | solution.py:28
  104.2 7.5 %copy-start.4 = (f32[1,16,8,4,128]{4,3,2,1,0:T(4,128)S(1)}, f32[1,16,8,4,128]{4,3,2,1,0:T(4,128)}, u32[]{:S(2)}) copy-start(f32[1,16,8,4,128]{4,3,2,1,0:T(4,128)} %stack.135) | copy-start | bytes 786436
  109.1 15.4 %collective-permute-start.14 = (f32[2,2,16,10,1]{4,3,2,1,0:T(8,128)}, f32[2,2,16,10,1]{4,3,2,1,0:T(8,128)}, u32[]{:S(2)}, u32[]{:S(2)}) collective-permute-start(f32[2,2,16,10,1]{4,3,2,1,0:T(8,128)} %get-tuple-element.28), channel_id=1, source_target_pairs={{0,1},{1,2},{2,3},{3,4},{4,5},{5,6},{6,7},{7,0},{8,9},{9,10},{10,1... | collective-permute-start | bytes 7688 | tf_op jit(solution)/shard_map/ppermute | solution.py:25
  109.1 15.4 %collective-permute-start.15 = (f32[2,2,16,10,1]{4,3,2,1,0:T(8,128)}, f32[2,2,16,10,1]{4,3,2,1,0:T(8,128)}, u32[]{:S(2)}, u32[]{:S(2)}) collective-permute-start(f32[2,2,16,10,1]{4,3,2,1,0:T(8,128)} %get-tuple-element.29), channel_id=1, source_target_pairs={{1,0},{2,1},{3,2},{4,3},{5,4},{6,5},{7,6},{0,7},{9,8},{10,9},{11,1... | collective-permute-start | bytes 7688 | tf_op jit(solution)/shard_map/ppermute | solution.py:28
  111.8 12.7 %copy-start.1 = (f32[2,16,8,4,128]{4,3,2,1,0:T(4,128)}, f32[2,16,8,4,128]{4,3,2,1,0:T(4,128)S(1)}, u32[]{:S(2)}) copy-start(f32[2,16,8,4,128]{4,3,2,1,0:T(4,128)S(1)} %constant_dynamic-update-slice_fusion) | copy-start | bytes 1572868
  (3 other events, 7.8 us)
where the time goes:
time: 176 us
  waiting for transfers between devices  64.3 us (37%)
  blocking collectives  38.9 us (22%)
  starting transfers between devices  31.4 us (18%)
  other arithmetic  29.2 us (17%)
  local copies, waits for them, and re-layouts  10.3 us (6%)
    ppermute x8, waiting for transfers between devices, extended(): lax.ppermute(lax.slice_in_dim(block, block.shape[dim] - width, None, axis...  52.5 us
    psum x1, blocking collectives, local(): summed = lax.psum(jnp.stack(partials), ('gx', 'gy'))  38.9 us
    ppermute x8, starting transfers between devices, extended(): lax.ppermute(lax.slice_in_dim(block, 0, width, axis=dim), axis, backward)  21 us
    all_to_all x1, waiting for transfers between devices, local(): lax.all_to_all(outgoing, 'gy', split_axis=0, concat_axis=0, tiled=True)  8.99 us
    concatenate x4, other arithmetic, extended(): block = jnp.concatenate([low, block, high], axis=dim)  7.79 us
    mul x8, other arithmetic, hamilton(): out_real.append(result_real * factor)  7.05 us
    another operation x9, local copies, waits for them, and re-layouts, hamilton(): return (jnp.stack(out_real), jnp.stack(out_imag))  6.65 us
    all_to_all x1, starting transfers between devices, local(): lax.all_to_all(outgoing, 'gy', split_axis=0, concat_axis=0, tiled=True)  5.2 us
  transfers between devices with their start and end apart: 17, of which 13 were waited for; matrix products, arithmetic and copies ran while one was open for 4% of the time, Pallas kernels for 0%

commit v1 on v0

--- a/solution.py
+++ b/solution.py
@@ -135,7 +135,9 @@
         previous_real, previous_imag = (current_real, current_imag)
         current_real, current_imag = (next_real, next_imag)
         record(current_real)
-    summed = lax.psum(jnp.stack(partials), ("gx", "gy"))
+    summed = jnp.stack(partials)
+    for name in ("gx", "gy"):
+        summed = lax.psum(summed, name)
     return (jnp.stack(locals_list), summed / sites_total)
 
 

time: 176 us -> 160 us (0.909)
  blocking collectives: 38.9 us -> 22.3 us
    psum x1 -> x2, blocking collectives: 38.9 us -> 22.3 us  [local(): summed = lax.psum(summed, name)]
  transfers between devices with their start and end apart: 17 -> 17, of which waited for: 13 -> 13; matrix products, arithmetic and copies ran while one was open for 4% -> 5% of each run, Pallas kernels for 0% -> 0%
where the time goes in v1:
time: 160 us; the launch traced here: 159 us
  waiting for transfers between devices  64.2 us (40%)
  starting transfers between devices  31.4 us (20%)
  other arithmetic  29.2 us (18%)
  blocking collectives  22.3 us (14%)
  local copies, waits for them, and re-layouts  10.4 us (6%)
    ppermute x8, waiting for transfers between devices, extended(): lax.ppermute(lax.slice_in_dim(block, block.shape[dim] - width, None, axis...  52.4 us
    psum x2, blocking collectives, local(): summed = lax.psum(summed, name)  22.3 us
    ppermute x8, starting transfers between devices, extended(): lax.ppermute(lax.slice_in_dim(block, 0, width, axis=dim), axis, backward)  21 us
    all_to_all x1, waiting for transfers between devices, local(): lax.all_to_all(outgoing, 'gy', split_axis=0, concat_axis=0, tiled=True)  9 us
    concatenate x4, other arithmetic, extended(): block = jnp.concatenate([low, block, high], axis=dim)  7.79 us
    mul x8, other arithmetic, hamilton(): out_real.append(result_real * factor)  7.05 us
    another operation x9, local copies, waits for them, and re-layouts, hamilton(): return (jnp.stack(out_real), jnp.stack(out_imag))  6.7 us
    all_to_all x1, starting transfers between devices, local(): lax.all_to_all(outgoing, 'gy', split_axis=0, concat_axis=0, tiled=True)  5.2 us
  transfers between devices with their start and end apart: 17, of which 13 were waited for; matrix products, arithmetic and copies ran while one was open for 5% of the time, Pallas kernels for 0%

profile of v1, /device:TPU:0, one launch (start us, length us, event | category | flops | bytes accessed | tf_op | source)
XLA Modules:
  0.0 159.4 jit_solution(12380930422159634014)
XLA Ops:
  2.9 5.2 %all-to-all-start = ((bf16[8,2,16,8,128]{4,3,2,1,0:T(8,128)(2,1)}), bf16[8,2,16,8,128]{4,3,2,1,0:T(8,128)(2,1)S(1)}, u32[]{:S(2)}, u32[]{:S(2)}) async-start(bf16[8,2,16,8,128]{4,3,2,1,0:T(8,128)(2,1)} %copy.10), calls=%async_computation | async-start | bytes 1048576 | tf_op jit(solution)/shard_map/all_to_all | solution.py:90
  8.8 9.0 %all-to-all-done = bf16[8,2,16,8,128]{4,3,2,1,0:T(8,128)(2,1)S(1)} async-done(((bf16[8,2,16,8,128]{4,3,2,1,0:T(8,128)(2,1)}), bf16[8,2,16,8,128]{4,3,2,1,0:T(8,128)(2,1)S(1)}, u32[]{:S(2)}, u32[]{:S(2)}) %all-to-all-start) | async-done | bytes 524320 | tf_op jit(solution)/shard_map/all_to_all | solution.py:90
  20.3 2.2 %collective-permute-start.1 = (f32[1,2,16,1,512]{4,3,2,1,0:T(1,128)S(1)}, f32[1,2,16,1,512]{4,3,2,1,0:T(1,128)S(1)}, u32[]{:S(2)}, u32[]{:S(2)}) collective-permute-start(f32[1,2,16,1,512]{4,3,2,1,0:T(1,128)S(1)} %get-tuple-element.54), channel_id=1, source_target_pairs={{8,0},{16,8},{24,16},{0,24},{9,1},{17,9},{25,17},{1,25},{10,2},{18... | collective-permute-start | bytes 196616 | tf_op jit(solution)/shard_map/ppermute | solution.py:28
  22.5 2.3 %collective-permute-done = f32[1,2,16,1,512]{4,3,2,1,0:T(1,128)S(1)} collective-permute-done((f32[1,2,16,1,512]{4,3,2,1,0:T(1,128)S(1)}, f32[1,2,16,1,512]{4,3,2,1,0:T(1,128)S(1)}, u32[]{:S(2)}, u32[]{:S(2)}) %collective-permute-start) | collective-permute-done | bytes 65568 | tf_op jit(solution)/shard_map/ppermute | solution.py:25
  25.5 2.6 %collective-permute-start.3 = (f32[1,2,16,10,1]{4,3,2,1,0:T(8,128)S(1)}, f32[1,2,16,10,1]{4,3,2,1,0:T(8,128)S(1)}, u32[]{:S(2)}, u32[]{:S(2)}) collective-permute-start(f32[1,2,16,10,1]{4,3,2,1,0:T(8,128)S(1)} %get-tuple-element.48), channel_id=1, source_target_pairs={{1,0},{2,1},{3,2},{4,3},{5,4},{6,5},{7,6},{0,7},{9,8},{10,9},{11,1... | collective-permute-start | bytes 3848 | tf_op jit(solution)/shard_map/ppermute | solution.py:28
  28.1 6.8 %collective-permute-done.2 = f32[1,2,16,10,1]{4,3,2,1,0:T(8,128)S(1)} collective-permute-done((f32[1,2,16,10,1]{4,3,2,1,0:T(8,128)S(1)}, f32[1,2,16,10,1]{4,3,2,1,0:T(8,128)S(1)}, u32[]{:S(2)}, u32[]{:S(2)}) %collective-permute-start.2) | collective-permute-done | bytes 1312 | tf_op jit(solution)/shard_map/ppermute | solution.py:25
  38.0 3.2 %collective-permute-start.5 = (f32[2,2,16,1,512]{4,3,2,1,0:T(1,128)S(1)}, f32[2,2,16,1,512]{4,3,2,1,0:T(1,128)S(1)}, u32[]{:S(2)}, u32[]{:S(2)}) collective-permute-start(f32[2,2,16,1,512]{4,3,2,1,0:T(1,128)S(1)} %get-tuple-element.46), channel_id=1, source_target_pairs={{8,0},{16,8},{24,16},{0,24},{9,1},{17,9},{25,17},{1,25},{10,2},{18... | collective-permute-start | bytes 393224 | tf_op jit(solution)/shard_map/ppermute | solution.py:28
  41.2 4.0 %collective-permute-done.4 = f32[2,2,16,1,512]{4,3,2,1,0:T(1,128)S(1)} collective-permute-done((f32[2,2,16,1,512]{4,3,2,1,0:T(1,128)S(1)}, f32[2,2,16,1,512]{4,3,2,1,0:T(1,128)S(1)}, u32[]{:S(2)}, u32[]{:S(2)}) %collective-permute-start.4) | collective-permute-done | bytes 131104 | tf_op jit(solution)/shard_map/ppermute | solution.py:25
  45.8 2.6 %collective-permute-start.7 = (f32[2,2,16,10,1]{4,3,2,1,0:T(8,128)S(1)}, f32[2,2,16,10,1]{4,3,2,1,0:T(8,128)S(1)}, u32[]{:S(2)}, u32[]{:S(2)}) collective-permute-start(f32[2,2,16,10,1]{4,3,2,1,0:T(8,128)S(1)} %get-tuple-element.33), channel_id=1, source_target_pairs={{1,0},{2,1},{3,2},{4,3},{5,4},{6,5},{7,6},{0,7},{9,8},{10,9},{11,1... | collective-permute-start | bytes 7688 | tf_op jit(solution)/shard_map/ppermute | solution.py:28
  48.5 11.6 %collective-permute-done.6 = f32[2,2,16,10,1]{4,3,2,1,0:T(8,128)S(1)} collective-permute-done((f32[2,2,16,10,1]{4,3,2,1,0:T(8,128)S(1)}, f32[2,2,16,10,1]{4,3,2,1,0:T(8,128)S(1)}, u32[]{:S(2)}, u32[]{:S(2)}) %collective-permute-start.6) | collective-permute-done | bytes 2592 | tf_op jit(solution)/shard_map/ppermute | solution.py:25
  65.9 2.1 %collective-permute-start.8 = (f32[2,2,16,1,512]{4,3,2,1,0:T(1,128)S(1)}, f32[2,2,16,1,512]{4,3,2,1,0:T(1,128)S(1)}, u32[]{:S(2)}, u32[]{:S(2)}) collective-permute-start(f32[2,2,16,1,512]{4,3,2,1,0:T(1,128)S(1)} %get-tuple-element.43), channel_id=1, source_target_pairs={{0,8},{8,16},{16,24},{24,0},{1,9},{9,17},{17,25},{25,1},{2,10},{10... | collective-permute-start | bytes 393224 | tf_op jit(solution)/shard_map/ppermute | solution.py:25
  69.8 4.4 %collective-permute-done.8 = f32[2,2,16,1,512]{4,3,2,1,0:T(1,128)S(1)} collective-permute-done((f32[2,2,16,1,512]{4,3,2,1,0:T(1,128)S(1)}, f32[2,2,16,1,512]{4,3,2,1,0:T(1,128)S(1)}, u32[]{:S(2)}, u32[]{:S(2)}) %collective-permute-start.8) | collective-permute-done | bytes 131104 | tf_op jit(solution)/shard_map/ppermute | solution.py:25
  74.2 1.9 %collective-permute-done.9 = f32[2,2,16,1,512]{4,3,2,1,0:T(1,128)S(1)} collective-permute-done((f32[2,2,16,1,512]{4,3,2,1,0:T(1,128)S(1)}, f32[2,2,16,1,512]{4,3,2,1,0:T(1,128)S(1)}, u32[]{:S(2)}, u32[]{:S(2)}) %collective-permute-start.9) | collective-permute-done | bytes 131104 | tf_op jit(solution)/shard_map/ppermute | solution.py:28
  76.5 2.6 %collective-permute-start.11 = (f32[2,2,16,10,1]{4,3,2,1,0:T(8,128)S(1)}, f32[2,2,16,10,1]{4,3,2,1,0:T(8,128)S(1)}, u32[]{:S(2)}, u32[]{:S(2)}) collective-permute-start(f32[2,2,16,10,1]{4,3,2,1,0:T(8,128)S(1)} %get-tuple-element.31), channel_id=1, source_target_pairs={{1,0},{2,1},{3,2},{4,3},{5,4},{6,5},{7,6},{0,7},{9,8},{10,9},{11,1... | collective-permute-start | bytes 7688 | tf_op jit(solution)/shard_map/ppermute | solution.py:28
  79.2 12.5 %collective-permute-done.10 = f32[2,2,16,10,1]{4,3,2,1,0:T(8,128)S(1)} collective-permute-done((f32[2,2,16,10,1]{4,3,2,1,0:T(8,128)S(1)}, f32[2,2,16,10,1]{4,3,2,1,0:T(8,128)S(1)}, u32[]{:S(2)}, u32[]{:S(2)}) %collective-permute-start.10) | collective-permute-done | bytes 2592 | tf_op jit(solution)/shard_map/ppermute | solution.py:25
  98.8 3.2 %collective-permute-start.13 = (f32[2,2,16,1,512]{4,3,2,1,0:T(1,128)}, f32[2,2,16,1,512]{4,3,2,1,0:T(1,128)}, u32[]{:S(2)}, u32[]{:S(2)}) collective-permute-start(f32[2,2,16,1,512]{4,3,2,1,0:T(1,128)} %get-tuple-element.42), channel_id=1, source_target_pairs={{8,0},{16,8},{24,16},{0,24},{9,1},{17,9},{25,17},{1,25},{10,2},{18... | collective-permute-start | bytes 393224 | tf_op jit(solution)/shard_map/ppermute | solution.py:28
  107.0 2.1 %pad_maximum_fusion.7 = (f32[2,2,16,10,1]{4,3,2,1,0:T(8,128)}, f32[2,2,16,10,1]{4,3,2,1,0:T(8,128)}) fusion(f32[2,2,16,1,512]{4,3,2,1,0:T(1,128)} %collective-permute-done.13, f32[2,2,16,1,512]{4,3,2,1,0:T(1,128)} %collective-permute-done.12, f32[1,2,16,8,512]{4,3,2,1,0:T(8,128)S(1)} %fusion.5, f32[1,2,16,8,512]{4,3,2,1,0:T(8,128)S(1)} %fusion.4), kind=kLoop, calls=%fused_computation.23 | loop fusion | flops 3840 | bytes 1315840 | tf_op jit(solution)/shard_map/slice | solution.py:26
  109.1 2.6 %collective-permute-start.15 = (f32[2,2,16,10,1]{4,3,2,1,0:T(8,128)}, f32[2,2,16,10,1]{4,3,2,1,0:T(8,128)}, u32[]{:S(2)}, u32[]{:S(2)}) collective-permute-start(f32[2,2,16,10,1]{4,3,2,1,0:T(8,128)} %get-tuple-element.29), channel_id=1, source_target_pairs={{1,0},{2,1},{3,2},{4,3},{5,4},{6,5},{7,6},{0,7},{9,8},{10,9},{11,1... | collective-permute-start | bytes 7688 | tf_op jit(solution)/shard_map/ppermute | solution.py:28
  115.1 9.4 %collective-permute-done.14 = f32[2,2,16,10,1]{4,3,2,1,0:T(8,128)} collective-permute-done((f32[2,2,16,10,1]{4,3,2,1,0:T(8,128)}, f32[2,2,16,10,1]{4,3,2,1,0:T(8,128)}, u32[]{:S(2)}, u32[]{:S(2)}) %collective-permute-start.14) | collective-permute-done | bytes 2592 | tf_op jit(solution)/shard_map/ppermute | solution.py:25
  124.5 3.1 %pad_maximum_fusion.2 = f32[2,2,16,10,514]{4,3,2,1,0:T(8,128)S(1)} fusion(f32[2,2,16,10,1]{4,3,2,1,0:T(8,128)} %collective-permute-done.15, f32[2,2,16,1,512]{4,3,2,1,0:T(1,128)} %collective-permute-done.13, f32[1,2,16,8,512]{4,3,2,1,0:T(8,128)S(1)} %fusion.5, f32[1,2,16,8,512]{4,3,2,1,0:T(8,128)S(1)} %fusion.4, ...), kind=kLoop, calls=%fused_computation.2 | loop fusion | flops 1644800 | bytes 2631680 | tf_op jit(solution)/shard_map/concatenate | solution.py:29
  129.5 2.4 %fusion.14 = f32[16,8,512]{2,1,0:T(8,128)} fusion(f32[16,10,514]{2,1,0:T(8,128)S(1)} %get-tuple-element.17, f32[16,10,514]{2,1,0:T(8,128)S(1)} %get-tuple-element.18, f32[16,10,514]{2,1,0:T(8,128)S(1)} %get-tuple-element.19, f32[8,512]{1,0:T(8,128)S(1)} %get-tuple-element.60, f32[8,512]{1,0:T(8,128)} %copy-done.5), kind=kLoop, calls=%fused_computation.58 | loop fusion | flops 1310720 | bytes 4489216 | tf_op jit(solution)/shard_map/mul | solution.py:65
  133.0 2.0 %fusion.38 = (f32[16]{0:T(128)S(1)}, f32[2,8,4,128]{3,2,1,0:T(4,128)S(1)}, f32[2,16,8,4,128]{4,3,2,1,0:T(4,128)S(1)}, f32[2,16,8,4,128]{4,3,2,1,0:T(4,128)S(1)}, f32[2,16,8,4,128]{4,3,2,1,0:T(4,128)S(1)}) fusion(f32[2,16,8,4,128]{4,3,2,1,0:T(4,128)S(1)} %copy-done.2, f32[2,16,8,4,128]{4,3,2,1,0:T(4,128)S(1)} %convolution_bitcast_fusion, ...), kind=kLoop, calls=%fused_computation.148 | loop fusion | flops 2088944 | bytes 4259904 | tf_op jit(solution)/shard_map/reduce_sum | solution.py:122
  135.7 10.6 %psum.14 = f32[4,16]{1,0:T(4,128)S(1)} all-reduce(f32[4,16]{1,0:T(4,128)S(1)} %pad_maximum_fusion.26), channel_id=1, replica_groups=mesh['gx'=4,'gy'=8] {'gx'}, use_global_device_ids=true, to_apply=%region_9.10 | all-reduce | flops 64 | bytes 512 | tf_op jit(solution)/shard_map/psum | solution.py:140
  146.2 11.8 %psum.15 = f32[4,16]{1,0:T(4,128)S(1)} all-reduce(f32[4,16]{1,0:T(4,128)S(1)} %psum.14), channel_id=1, replica_groups=mesh['gx'=4,'gy'=8] {'gy'}, use_global_device_ids=true, to_apply=%region_10.11 | all-reduce | flops 64 | bytes 512 | tf_op jit(solution)/shard_map/psum | solution.py:140
  (104 shorter events, 37.9 us)
Async XLA Ops:
  0.6 7.5 %copy-start.9 = (s32[32]{0:T(128)S(1)}, s32[32]{0:T(128)}, u32[]{:S(2)}) copy-start(s32[32]{0:T(128)} %param.7) | copy-start | bytes 388
  0.7 7.6 %copy-start.7 = (s32[2,8,512]{2,1,0:T(8,128)S(1)}, s32[2,8,512]{2,1,0:T(8,128)}, u32[]{:S(2)}) copy-start(s32[2,8,512]{2,1,0:T(8,128)} %param.6) | copy-start | bytes 98308
  2.0 20.5 %copy-start.8 = (f32[2,8,512]{2,1,0:T(8,128)S(1)}, f32[2,8,512]{2,1,0:T(8,128)}, u32[]{:S(2)}) copy-start(f32[2,8,512]{2,1,0:T(8,128)} %param.5) | copy-start | bytes 98308
  2.9 14.9 %all-to-all-start = ((bf16[8,2,16,8,128]{4,3,2,1,0:T(8,128)(2,1)}), bf16[8,2,16,8,128]{4,3,2,1,0:T(8,128)(2,1)S(1)}, u32[]{:S(2)}, u32[]{:S(2)}) async-start(bf16[8,2,16,8,128]{4,3,2,1,0:T(8,128)(2,1)} %copy.10), calls=%async_computation | async-start | bytes 1048576 | tf_op jit(solution)/shard_map/all_to_all | solution.py:90
  18.6 6.2 %collective-permute-start = (f32[1,2,16,1,512]{4,3,2,1,0:T(1,128)S(1)}, f32[1,2,16,1,512]{4,3,2,1,0:T(1,128)S(1)}, u32[]{:S(2)}, u32[]{:S(2)}) collective-permute-start(f32[1,2,16,1,512]{4,3,2,1,0:T(1,128)S(1)} %get-tuple-element.53), channel_id=1, source_target_pairs={{0,8},{8,16},{16,24},{24,0},{1,9},{9,17},{17,25},{25,1},{2,10},{10... | collective-permute-start | bytes 196616 | tf_op jit(solution)/shard_map/ppermute | solution.py:25
  20.3 5.0 %collective-permute-start.1 = (f32[1,2,16,1,512]{4,3,2,1,0:T(1,128)S(1)}, f32[1,2,16,1,512]{4,3,2,1,0:T(1,128)S(1)}, u32[]{:S(2)}, u32[]{:S(2)}) collective-permute-start(f32[1,2,16,1,512]{4,3,2,1,0:T(1,128)S(1)} %get-tuple-element.54), channel_id=1, source_target_pairs={{8,0},{16,8},{24,16},{0,24},{9,1},{17,9},{25,17},{1,25},{10,2},{18... | collective-permute-start | bytes 196616 | tf_op jit(solution)/shard_map/ppermute | solution.py:28
  22.5 73.8 %copy-start.5 = (f32[8,512]{1,0:T(8,128)}, f32[8,512]{1,0:T(8,128)S(1)}, u32[]{:S(2)}) copy-start(f32[8,512]{1,0:T(8,128)S(1)} %get-tuple-element.66) | copy-start | bytes 49156
  25.4 9.6 %collective-permute-start.2 = (f32[1,2,16,10,1]{4,3,2,1,0:T(8,128)S(1)}, f32[1,2,16,10,1]{4,3,2,1,0:T(8,128)S(1)}, u32[]{:S(2)}, u32[]{:S(2)}) collective-permute-start(f32[1,2,16,10,1]{4,3,2,1,0:T(8,128)S(1)} %get-tuple-element.47), channel_id=1, source_target_pairs={{0,1},{1,2},{2,3},{3,4},{4,5},{5,6},{6,7},{7,0},{8,9},{9,10},{10,1... | collective-permute-start | bytes 3848 | tf_op jit(solution)/shard_map/ppermute | solution.py:25
  25.5 9.5 %collective-permute-start.3 = (f32[1,2,16,10,1]{4,3,2,1,0:T(8,128)S(1)}, f32[1,2,16,10,1]{4,3,2,1,0:T(8,128)S(1)}, u32[]{:S(2)}, u32[]{:S(2)}) collective-permute-start(f32[1,2,16,10,1]{4,3,2,1,0:T(8,128)S(1)} %get-tuple-element.48), channel_id=1, source_target_pairs={{1,0},{2,1},{3,2},{4,3},{5,4},{6,5},{7,6},{0,7},{9,8},{10,9},{11,1... | collective-permute-start | bytes 3848 | tf_op jit(solution)/shard_map/ppermute | solution.py:28
  37.3 7.9 %collective-permute-start.4 = (f32[2,2,16,1,512]{4,3,2,1,0:T(1,128)S(1)}, f32[2,2,16,1,512]{4,3,2,1,0:T(1,128)S(1)}, u32[]{:S(2)}, u32[]{:S(2)}) collective-permute-start(f32[2,2,16,1,512]{4,3,2,1,0:T(1,128)S(1)} %get-tuple-element.45), channel_id=1, source_target_pairs={{0,8},{8,16},{16,24},{24,0},{1,9},{9,17},{17,25},{25,1},{2,10},{10... | collective-permute-start | bytes 393224 | tf_op jit(solution)/shard_map/ppermute | solution.py:25
  38.0 7.4 %collective-permute-start.5 = (f32[2,2,16,1,512]{4,3,2,1,0:T(1,128)S(1)}, f32[2,2,16,1,512]{4,3,2,1,0:T(1,128)S(1)}, u32[]{:S(2)}, u32[]{:S(2)}) collective-permute-start(f32[2,2,16,1,512]{4,3,2,1,0:T(1,128)S(1)} %get-tuple-element.46), channel_id=1, source_target_pairs={{8,0},{16,8},{24,16},{0,24},{9,1},{17,9},{25,17},{1,25},{10,2},{18... | collective-permute-start | bytes 393224 | tf_op jit(solution)/shard_map/ppermute | solution.py:28
  45.8 14.3 %collective-permute-start.6 = (f32[2,2,16,10,1]{4,3,2,1,0:T(8,128)S(1)}, f32[2,2,16,10,1]{4,3,2,1,0:T(8,128)S(1)}, u32[]{:S(2)}, u32[]{:S(2)}) collective-permute-start(f32[2,2,16,10,1]{4,3,2,1,0:T(8,128)S(1)} %get-tuple-element.32), channel_id=1, source_target_pairs={{0,1},{1,2},{2,3},{3,4},{4,5},{5,6},{6,7},{7,0},{8,9},{9,10},{10,1... | collective-permute-start | bytes 7688 | tf_op jit(solution)/shard_map/ppermute | solution.py:25
  45.8 14.2 %collective-permute-start.7 = (f32[2,2,16,10,1]{4,3,2,1,0:T(8,128)S(1)}, f32[2,2,16,10,1]{4,3,2,1,0:T(8,128)S(1)}, u32[]{:S(2)}, u32[]{:S(2)}) collective-permute-start(f32[2,2,16,10,1]{4,3,2,1,0:T(8,128)S(1)} %get-tuple-element.33), channel_id=1, source_target_pairs={{1,0},{2,1},{3,2},{4,3},{5,4},{6,5},{7,6},{0,7},{9,8},{10,9},{11,1... | collective-permute-start | bytes 7688 | tf_op jit(solution)/shard_map/ppermute | solution.py:28
  65.9 8.3 %collective-permute-start.8 = (f32[2,2,16,1,512]{4,3,2,1,0:T(1,128)S(1)}, f32[2,2,16,1,512]{4,3,2,1,0:T(1,128)S(1)}, u32[]{:S(2)}, u32[]{:S(2)}) collective-permute-start(f32[2,2,16,1,512]{4,3,2,1,0:T(1,128)S(1)} %get-tuple-element.43), channel_id=1, source_target_pairs={{0,8},{8,16},{16,24},{24,0},{1,9},{9,17},{17,25},{25,1},{2,10},{10... | collective-permute-start | bytes 393224 | tf_op jit(solution)/shard_map/ppermute | solution.py:25
  68.0 8.1 %collective-permute-start.9 = (f32[2,2,16,1,512]{4,3,2,1,0:T(1,128)S(1)}, f32[2,2,16,1,512]{4,3,2,1,0:T(1,128)S(1)}, u32[]{:S(2)}, u32[]{:S(2)}) collective-permute-start(f32[2,2,16,1,512]{4,3,2,1,0:T(1,128)S(1)} %get-tuple-element.44), channel_id=1, source_target_pairs={{8,0},{16,8},{24,16},{0,24},{9,1},{17,9},{25,17},{1,25},{10,2},{18... | collective-permute-start | bytes 393224 | tf_op jit(solution)/shard_map/ppermute | solution.py:28
  76.5 15.2 %collective-permute-start.10 = (f32[2,2,16,10,1]{4,3,2,1,0:T(8,128)S(1)}, f32[2,2,16,10,1]{4,3,2,1,0:T(8,128)S(1)}, u32[]{:S(2)}, u32[]{:S(2)}) collective-permute-start(f32[2,2,16,10,1]{4,3,2,1,0:T(8,128)S(1)} %get-tuple-element.30), channel_id=1, source_target_pairs={{0,1},{1,2},{2,3},{3,4},{4,5},{5,6},{6,7},{7,0},{8,9},{9,10},{10,1... | collective-permute-start | bytes 7688 | tf_op jit(solution)/shard_map/ppermute | solution.py:25
  76.5 15.1 %collective-permute-start.11 = (f32[2,2,16,10,1]{4,3,2,1,0:T(8,128)S(1)}, f32[2,2,16,10,1]{4,3,2,1,0:T(8,128)S(1)}, u32[]{:S(2)}, u32[]{:S(2)}) collective-permute-start(f32[2,2,16,10,1]{4,3,2,1,0:T(8,128)S(1)} %get-tuple-element.31), channel_id=1, source_target_pairs={{1,0},{2,1},{3,2},{4,3},{5,4},{6,5},{7,6},{0,7},{9,8},{10,9},{11,1... | collective-permute-start | bytes 7688 | tf_op jit(solution)/shard_map/ppermute | solution.py:28
  97.2 4.9 %copy-start.6 = (f32[2,8,4,128]{3,1,2,0:T(8,128)S(1)}, f32[2,8,4,128]{3,1,2,0:T(8,128)}, u32[]{:S(2)}) copy-start(f32[2,8,4,128]{3,1,2,0:T(8,128)} %get-tuple-element.55) | copy-start | bytes 98308
  98.3 8.5 %collective-permute-start.12 = (f32[2,2,16,1,512]{4,3,2,1,0:T(1,128)}, f32[2,2,16,1,512]{4,3,2,1,0:T(1,128)}, u32[]{:S(2)}, u32[]{:S(2)}) collective-permute-start(f32[2,2,16,1,512]{4,3,2,1,0:T(1,128)} %get-tuple-element.41), channel_id=1, source_target_pairs={{0,8},{8,16},{16,24},{24,0},{1,9},{9,17},{17,25},{25,1},{2,10},{10... | collective-permute-start | bytes 393224 | tf_op jit(solution)/shard_map/ppermute | solution.py:25
  98.8 8.1 %collective-permute-start.13 = (f32[2,2,16,1,512]{4,3,2,1,0:T(1,128)}, f32[2,2,16,1,512]{4,3,2,1,0:T(1,128)}, u32[]{:S(2)}, u32[]{:S(2)}) collective-permute-start(f32[2,2,16,1,512]{4,3,2,1,0:T(1,128)} %get-tuple-element.42), channel_id=1, source_target_pairs={{8,0},{16,8},{24,16},{0,24},{9,1},{17,9},{25,17},{1,25},{10,2},{18... | collective-permute-start | bytes 393224 | tf_op jit(solution)/shard_map/ppermute | solution.py:28
  104.3 7.5 %copy-start.4 = (f32[1,16,8,4,128]{4,3,2,1,0:T(4,128)S(1)}, f32[1,16,8,4,128]{4,3,2,1,0:T(4,128)}, u32[]{:S(2)}) copy-start(f32[1,16,8,4,128]{4,3,2,1,0:T(4,128)} %stack.135) | copy-start | bytes 786436
  109.1 15.4 %collective-permute-start.14 = (f32[2,2,16,10,1]{4,3,2,1,0:T(8,128)}, f32[2,2,16,10,1]{4,3,2,1,0:T(8,128)}, u32[]{:S(2)}, u32[]{:S(2)}) collective-permute-start(f32[2,2,16,10,1]{4,3,2,1,0:T(8,128)} %get-tuple-element.28), channel_id=1, source_target_pairs={{0,1},{1,2},{2,3},{3,4},{4,5},{5,6},{6,7},{7,0},{8,9},{9,10},{10,1... | collective-permute-start | bytes 7688 | tf_op jit(solution)/shard_map/ppermute | solution.py:25
  109.1 15.4 %collective-permute-start.15 = (f32[2,2,16,10,1]{4,3,2,1,0:T(8,128)}, f32[2,2,16,10,1]{4,3,2,1,0:T(8,128)}, u32[]{:S(2)}, u32[]{:S(2)}) collective-permute-start(f32[2,2,16,10,1]{4,3,2,1,0:T(8,128)} %get-tuple-element.29), channel_id=1, source_target_pairs={{1,0},{2,1},{3,2},{4,3},{5,4},{6,5},{7,6},{0,7},{9,8},{10,9},{11,1... | collective-permute-start | bytes 7688 | tf_op jit(solution)/shard_map/ppermute | solution.py:28
  111.8 12.7 %copy-start.1 = (f32[2,16,8,4,128]{4,3,2,1,0:T(4,128)}, f32[2,16,8,4,128]{4,3,2,1,0:T(4,128)S(1)}, u32[]{:S(2)}) copy-start(f32[2,16,8,4,128]{4,3,2,1,0:T(4,128)S(1)} %constant_dynamic-update-slice_fusion) | copy-start | bytes 1572868
  (3 other events, 7.8 us)
